TPU v7x, 32 devices: a whole 2x2x4 slice. The times are simulated.
32 devices in a mesh: rows: 8 (over y, x, core), sub: 4 (over z).
Axes of the slice: x: 2, y: 2, z: 4, core: 2. Of those that a mesh axis runs over, the one named last changes fastest.
Arguments:
- u_fem: float32 [120, 524288], P(None, ('rows', 'sub')), may hold values from -600 to 600
- resid_fem: float32 [1, 524288], P(None, ('rows', 'sub')), may hold values from -60 to 60
- slot_map: int32 [32, 32], P(('rows', 'sub')), may hold values from 0 to 31, as said below
- restart: float32 [120, 40], replicated, may hold values from -0.5 to 0.5
- coeff: float32 [3, 120, 120], P(None, None, 'sub'), may hold values from -6 to 6
Outputs:
- new_basis: float32 [40, 524288], P(None, ('rows', 'sub'))
- next_vector: float32 [1, 524288], P(None, ('rows', 'sub'))
- new_coeff: float32 [3, 40, 120], replicated
Inputs may be any that keep to these rules, and one draw needn't show every extreme that they name: Each row of slot_map is a permutation of 0 to 31.
All inputs are finite; a program needn't handle non-finite values.
Results may differ from a plain program's by a relative error of at most 0.00015.
Values sent between devices are 32-bit elements; how exact they have to be, the bound alone decides.
A program may use at most 64 MiB of HBM per device.

v0:
```python
import jax
import jax.numpy as jnp
from jax import lax
from jax.sharding import PartitionSpec as P


def settle(values, source, dev_count):
    width = values.shape[0]
    block_len = values.shape[1] // dev_count
    blocks = values.reshape(width, dev_count, block_len)
    return jnp.take(blocks, source, axis=1).reshape(width, dev_count * block_len)


def local(u_fem, resid_fem, slot_map, restart, coeff):
    highest = lax.Precision.HIGHEST
    dev_count = lax.axis_size(("rows", "sub"))
    nrows_all = u_fem.shape[1] * dev_count
    source = jnp.argsort(slot_map[0])
    basis_rows, resid_row = (u_fem, resid_fem)
    gram_local = jnp.einsum("kn,jn->kj", basis_rows, basis_rows, precision=highest)
    inner_local = jnp.einsum("kn,n->k", basis_rows, resid_row[0], precision=highest)
    gram_sum = lax.psum(gram_local, ("rows", "sub"))
    chol_lower = jnp.linalg.cholesky(gram_sum / nrows_all)
    factor = lax.linalg.triangular_solve(
        chol_lower, restart, left_side=True, lower=True, transpose_a=True
    )
    new_rows = jnp.einsum("kp,kn->pn", factor, basis_rows, precision=highest)
    inner_prod = lax.psum(inner_local, ("rows", "sub"))
    half_solve = lax.linalg.triangular_solve(
        chol_lower, inner_prod[:, None], left_side=True, lower=True
    )
    proj_coef = (
        lax.linalg.triangular_solve(
            chol_lower, half_solve, left_side=True, lower=True, transpose_a=True
        )[:, 0]
        / nrows_all
    )
    remainder = resid_row - jnp.einsum("k,kn->n", proj_coef, basis_rows, precision=highest)[None, :]
    norm_sum = lax.psum(jnp.sum(remainder * remainder), ("rows", "sub"))
    next_row = remainder * lax.rsqrt(norm_sum / nrows_all + 1e-06)
    new_rows, next_row = (
        lax.all_to_all(new_rows, ("rows", "sub"), split_axis=1, concat_axis=1, tiled=True),
        lax.all_to_all(next_row, ("rows", "sub"), split_axis=1, concat_axis=1, tiled=True),
    )
    new_rows = settle(new_rows, source, dev_count)
    next_row = settle(next_row, source, dev_count)
    raised = jnp.dot(chol_lower, restart, precision=highest)
    coeff_all = lax.all_gather(coeff, "sub", axis=2, tiled=True)
    rotated = jnp.einsum("kp,ikm->ipm", raised, coeff_all, precision=highest)
    new_coeff = rotated * lax.rsqrt(jnp.mean(rotated * rotated) + 1e-06)
    return (new_rows, next_row, new_coeff)


def solution(mesh):
    in_specs = (
        P(None, ("rows", "sub")),
        P(None, ("rows", "sub")),
        P(("rows", "sub"), None),
        P(),
        P(None, None, "sub"),
    )
    out_specs = (P(None, ("rows", "sub")), P(None, ("rows", "sub")), P())
    return jax.shard_map(local, mesh=mesh, in_specs=in_specs, out_specs=out_specs, check_vma=False)
```

profile of v0, /device:TPU:0, one launch (start us, length us, event | category | flops | bytes accessed | tf_op | source)
XLA Modules:
  0.0 229.9 jit_solution(9403381852364649270)
XLA Ops:
  0.7 10.1 %fusion.16 = f32[120,120]{0,1:T(8,128)S(1)} fusion(f32[120,16384]{1,0:T(8,128)} %param.5), kind=kOutput, calls=%fused_computation.44 | convolution fusion | flops 2831155200 | bytes 7921920 | tf_op jit(solution)/shard_map/kn,jn->kj/dot_general | solution.py:20
  10.8 6.2 %convolution_bitcast_fusion.3 = f32[120]{0:T(128)S(1)} fusion(f32[120,16384]{1,0:T(8,128)S(1)} %copy-done.1, f32[1,16384]{1,0:T(1,128)S(1)} %copy-done.2), kind=kOutput, calls=%fused_computation.10 | convolution fusion | flops 23592960 | bytes 7930336 | tf_op jit(solution)/shard_map/kn,n->k/dot_general | solution.py:21
  16.9 42.8 %all-reduce = (f32[120,120]{0,1:T(8,128)S(1)}, f32[120]{0:T(128)S(1)}) all-reduce(f32[120,120]{0,1:T(8,128)S(1)} %fusion.16, f32[120]{0:T(128)S(1)} %convolution_bitcast_fusion.3), channel_id=1, replica_groups=mesh['rows'=8,'sub'=4] {'rows','sub'}, use_global_device_ids=true, to_apply=%region_1.2 | all-reduce | flops 14520 | bytes 116160 | tf_op jit(solution)/shard_map/psum | solution.py:22
  59.9 11.0 %cholesky.16 = f32[120,120]{1,0:T(8,128)S(1)} custom-call(f32[120,120]{1,0:T(8,128)S(1)} %fusion.9), custom_call_target="Cholesky" | custom-call | tf_op jit(solution)/shard_map/jit(cholesky)/cholesky | solution.py:23
  70.9 0.6 compare_reduce_fusion
  71.5 0.7 select_bitcast_fusion
  72.2 9.2 %custom-call.10 = f32[1,120,120]{1,2,0:T(8,128)S(1)} custom-call(f32[1,120,120]{2,1,0:T(8,128)S(1)} %select_bitcast_fusion), custom_call_target="InvertDiagBlocksLowerTriangular" | custom-call | tf_op jit(solution)/shard_map/triangular_solve | solution.py:24
  81.8 6.7 %multiply_reduce_fusion = (f32[]{:T(128)}, f32[1,16384]{1,0:T(1,128)S(1)}) fusion(f32[1,16384]{1,0:T(1,128)S(1)} %copy-done.2, f32[120,1]{0,1:T(1,128)S(1)} %fusion.1, f32[120,16384]{1,0:T(8,128)} %param.5), kind=kOutput, calls=%fused_computation.15 | convolution fusion | flops 23642112 | bytes 7995876 | tf_op jit(solution)/shard_map/k,kn->n/dot_general | solution.py:38
  88.5 40.3 %psum.23 = f32[]{:T(128)} all-reduce(f32[]{:T(128)} %get-tuple-element.7), channel_id=1, replica_groups=mesh['rows'=8,'sub'=4] {'rows','sub'}, use_global_device_ids=true, to_apply=%region_6.7 | all-reduce | flops 1 | bytes 8 | tf_op jit(solution)/shard_map/psum | solution.py:39
  129.5 0.7 broadcast_multiply_fusion
  130.1 5.4 %all-to-all-start.1 = ((f32[1,32,512]{2,0,1:T(1,128)}), f32[1,32,512]{2,0,1:T(1,128)S(1)}, u32[]{:S(2)}, u32[]{:S(2)}) async-start(f32[1,32,512]{2,0,1:T(1,128)} %bitcast.14), calls=%async_computation.1 | async-start | bytes 131072 | tf_op jit(solution)/shard_map/all_to_all | solution.py:43
  135.8 6.5 %fusion.17 = f32[40,16384]{1,0:T(8,128)S(1)} fusion(f32[120,40]{0,1:T(8,128)S(1)} %fusion.7, f32[120,16384]{1,0:T(8,128)} %param.5), kind=kOutput, calls=%fused_computation.45 | convolution fusion | flops 943718400 | bytes 10504960 | tf_op jit(solution)/shard_map/kp,kn->pn/dot_general | solution.py:27
  142.3 1.7 copy.36
  144.1 1.7 sort.17
  145.8 5.8 %all-to-all-start = ((f32[40,32,512]{2,0,1:T(8,128)}), f32[40,32,512]{2,0,1:T(8,128)S(1)}, u32[]{:S(2)}, u32[]{:S(2)}) async-start(f32[40,32,512]{2,0,1:T(8,128)} %bitcast.69), calls=%async_computation | async-start | bytes 5242880 | tf_op jit(solution)/shard_map/all_to_all | solution.py:42
  151.8 67.3 %all_gather.3 = f32[3,120,120]{1,0,2:T(4,128)S(1)} all-gather(f32[3,120,30]{1,0,2:T(4,128)S(1)} %copy.21), channel_id=1, replica_groups=mesh['rows'=8,'sub'=4] {'sub'}, dimensions={2}, use_global_device_ids=true | all-gather | bytes 216000 | tf_op jit(solution)/shard_map/all_gather | solution.py:48
  219.1 0.9 convolution_bitcast_fusion
  220.0 1.0 multiply_reduce_fusion.1
  221.9 0.6 multiply_bitcast_fusion
  222.5 0.6 gather_fusion.1
  223.2 0.7 broadcast_select_fusion.1
  223.9 2.2 gather_fusion
  226.2 2.1 copy.26
  228.2 1.7 broadcast_select_fusion
  (30 shorter events, 1.1 us)
Async XLA Ops:
  0.6 134.9 %copy-start = (f32[120,40]{0,1:T(8,128)S(1)}, f32[120,40]{0,1:T(8,128)}, u32[]{:S(2)}) copy-start(f32[120,40]{0,1:T(8,128)} %param.8) | copy-start | bytes 57604
  0.6 10.1 %copy-start.1 = (f32[120,16384]{1,0:T(8,128)S(1)}, f32[120,16384]{1,0:T(8,128)}, u32[]{:S(2)}) copy-start(f32[120,16384]{1,0:T(8,128)} %param.5) | copy-start | bytes 23592964
  0.7 10.1 %copy-start.2 = (f32[1,16384]{1,0:T(1,128)S(1)}, f32[1,16384]{1,0:T(1,128)}, u32[]{:S(2)}) copy-start(f32[1,16384]{1,0:T(1,128)} %param.6) | copy-start | bytes 196612
  130.1 15.6 %all-to-all-start.1 = ((f32[1,32,512]{2,0,1:T(1,128)}), f32[1,32,512]{2,0,1:T(1,128)S(1)}, u32[]{:S(2)}, u32[]{:S(2)}) async-start(f32[1,32,512]{2,0,1:T(1,128)} %bitcast.14), calls=%async_computation.1 | async-start | bytes 131072 | tf_op jit(solution)/shard_map/all_to_all | solution.py:43
  135.8 8.3 %copy-start.4 = (s32[1,32]{1,0:T(1,128)S(1)}, s32[1,32]{1,0:T(1,128)}, u32[]{:S(2)}) copy-start(s32[1,32]{1,0:T(1,128)} %param.7) | copy-start | bytes 388
  142.3 9.4 %copy-start.3 = (f32[3,120,30]{1,2,0:T(8,128)S(1)}, f32[3,120,30]{1,2,0:T(8,128)}, u32[]{:S(2)}) copy-start(f32[3,120,30]{1,2,0:T(8,128)} %param.9) | copy-start | bytes 129604
  145.8 78.2 %all-to-all-start = ((f32[40,32,512]{2,0,1:T(8,128)}), f32[40,32,512]{2,0,1:T(8,128)S(1)}, u32[]{:S(2)}, u32[]{:S(2)}) async-start(f32[40,32,512]{2,0,1:T(8,128)} %bitcast.69), calls=%async_computation | async-start | bytes 5242880 | tf_op jit(solution)/shard_map/all_to_all | solution.py:42
where the time goes:
time: 231 us; the launch traced here: 230 us
  blocking collectives  150 us (65%)
  matrix products  32 us (14%)
  other arithmetic  27 us (12%)
  starting transfers between devices  11.2 us (5%)
  local copies, waits for them, and re-layouts  7.06 us (3%)
    all_gather x1, blocking collectives, local(): coeff_all = lax.all_gather(coeff, 'sub', axis=2, tiled=True)  67.3 us
    psum x1, blocking collectives, local(): gram_sum = lax.psum(gram_local, ('rows', 'sub'))  42.8 us
    psum x1, blocking collectives, local(): norm_sum = lax.psum(jnp.sum(remainder * remainder), ('rows', 'sub'))  40.3 us
    another operation x3, other arithmetic, local(): chol_lower = jnp.linalg.cholesky(gram_sum / nrows_all)  11.6 us
    dot_general x1, matrix products, local(): jnp.einsum('kn,jn->kj', basis_rows, basis_rows, precision=highest)  10.1 us
    another operation x2, other arithmetic, local(): lax.linalg.triangular_solve(chol_lower, restart, left_side=True, lower=Tr...  9.85 us
    dot_general x1, matrix products, local(): jnp.einsum('k,kn->n', proj_coef, basis_rows, precision=highest)[None, :]  6.74 us
    dot_general x1, matrix products, local(): new_rows = jnp.einsum('kp,kn->pn', factor, basis_rows, precision=highest)  6.51 us
  transfers between devices with their start and end apart: 2, of which 0 were waited for; matrix products, arithmetic and copies ran while one was open for 6% of the time, Pallas kernels for 0%

commit v1 on v0

--- a/solution.py
+++ b/solution.py
@@ -19,7 +19,8 @@
     basis_rows, resid_row = (u_fem, resid_fem)
     gram_local = jnp.einsum("kn,jn->kj", basis_rows, basis_rows, precision=highest)
     inner_local = jnp.einsum("kn,n->k", basis_rows, resid_row[0], precision=highest)
-    gram_sum = lax.psum(gram_local, ("rows", "sub"))
+    parts = lax.all_gather(gram_local, ("rows", "sub"), axis=0, tiled=False)
+    gram_sum = parts.sum(axis=0)
     chol_lower = jnp.linalg.cholesky(gram_sum / nrows_all)
     factor = lax.linalg.triangular_solve(
         chol_lower, restart, left_side=True, lower=True, transpose_a=True

time: 231 us -> 253 us (1.095)
  between operations: 2.26 us -> 15.6 us
  waiting for transfers between devices: 0.01 us -> 6.92 us
  matrix products: 32 us -> 34.7 us
    all_gather x0 -> x1, waiting for transfers between devices: none -> 6.9 us  [local(): parts = lax.all_gather(gram_local, ('rows', 'sub'), axis=0, tiled=False)]
  transfers between devices with their start and end apart: 2 -> 3, of which waited for: 0 -> 1; matrix products, arithmetic and copies ran while one was open for 6% -> 9% of each run, Pallas kernels for 0% -> 0%
where the time goes in v1:
time: 253 us; the launch traced here: 252 us
  blocking collectives  148 us (58%)
  matrix products  34.7 us (14%)
  other arithmetic  28.6 us (11%)
  between operations  15.6 us (6%)
  starting transfers between devices  11.3 us (4%)
  local copies, waits for them, and re-layouts  6.97 us (3%)
  waiting for transfers between devices  6.92 us (3%)
    all_gather x1, blocking collectives, local(): coeff_all = lax.all_gather(coeff, 'sub', axis=2, tiled=True)  67.2 us
    psum x1, blocking collectives, local(): inner_prod = lax.psum(inner_local, ('rows', 'sub'))  42.1 us
    psum x1, blocking collectives, local(): norm_sum = lax.psum(jnp.sum(remainder * remainder), ('rows', 'sub'))  38.6 us
    another operation x3, other arithmetic, local(): chol_lower = jnp.linalg.cholesky(gram_sum / nrows_all)  11.6 us
    dot_general x1, matrix products, local(): jnp.einsum('kn,jn->kj', basis_rows, basis_rows, precision=highest)  10.5 us
    another operation x2, other arithmetic, local(): lax.linalg.triangular_solve(chol_lower, restart, left_side=True, lower=Tr...  9.85 us
    dot_general x1, matrix products, local(): jnp.einsum('kn,n->k', basis_rows, resid_row[0], precision=highest)  8.41 us
    all_gather x1, waiting for transfers between devices, local(): parts = lax.all_gather(gram_local, ('rows', 'sub'), axis=0, tiled=False)  6.9 us
  transfers between devices with their start and end apart: 3, of which 1 were waited for; matrix products, arithmetic and copies ran while one was open for 9% of the time, Pallas kernels for 0%

profile of v1, /device:TPU:0, one launch (start us, length us, event | category | flops | bytes accessed | tf_op | source)
XLA Modules:
  0.0 252.0 jit_solution(6336451378936123688)
XLA Ops:
  7.2 10.5 %fusion.16 = f32[120,120]{1,0:T(8,128)} fusion(f32[120,16384]{1,0:T(8,128)} %param.5), kind=kOutput, calls=%fused_computation.43 | convolution fusion | flops 2831155200 | bytes 7921920 | tf_op jit(solution)/shard_map/kn,jn->kj/dot_general | solution.py:20
  17.8 1.6 sort.17
  19.4 8.4 %convolution_bitcast_fusion.3 = f32[120]{0:T(128)S(1)} fusion(f32[120,16384]{1,0:T(8,128)} %param.5, f32[1,16384]{1,0:T(1,128)S(1)} %copy-done.1), kind=kOutput, calls=%fused_computation.10 | convolution fusion | flops 23592960 | bytes 7930336 | tf_op jit(solution)/shard_map/kn,n->k/dot_general | solution.py:21
  27.8 42.1 %psum.14 = f32[120]{0:T(128)S(1)} all-reduce(f32[120]{0:T(128)S(1)} %convolution_bitcast_fusion.3), channel_id=1, replica_groups=mesh['rows'=8,'sub'=4] {'rows','sub'}, use_global_device_ids=true, to_apply=%region_4.5 | all-reduce | flops 120 | bytes 960 | tf_op jit(solution)/shard_map/psum | solution.py:29
  70.0 6.9 %all-gather.3.cloned.1.call-done = f32[3840,120]{1,0:T(8,128)} async-done(((f32[120,120]{1,0:T(8,128)}), f32[3840,120]{1,0:T(8,128)}) %all-gather.3.cloned.1.call-update) | async-done | bytes 1843216 | tf_op jit(solution)/shard_map/all_gather | solution.py:22
  76.9 1.7 reduce_sum.29
  78.7 11.0 %cholesky.16 = f32[120,120]{1,0:T(8,128)S(1)} custom-call(f32[120,120]{1,0:T(8,128)S(1)} %fusion.9), custom_call_target="Cholesky" | custom-call | tf_op jit(solution)/shard_map/jit(cholesky)/cholesky | solution.py:24
  89.7 0.6 compare_reduce_fusion
  90.3 0.7 select_bitcast_fusion
  91.0 9.2 %custom-call.10 = f32[1,120,120]{1,2,0:T(8,128)S(1)} custom-call(f32[1,120,120]{2,1,0:T(8,128)S(1)} %select_bitcast_fusion), custom_call_target="InvertDiagBlocksLowerTriangular" | custom-call | tf_op jit(solution)/shard_map/triangular_solve | solution.py:25
  100.6 6.7 %multiply_reduce_fusion = (f32[]{:T(128)}, f32[1,16384]{1,0:T(1,128)S(1)}) fusion(f32[1,16384]{1,0:T(1,128)S(1)} %copy-done.1, f32[120,1]{0,1:T(1,128)S(1)} %fusion.1, f32[120,16384]{1,0:T(8,128)} %param.5), kind=kOutput, calls=%fused_computation.15 | convolution fusion | flops 23642112 | bytes 7995876 | tf_op jit(solution)/shard_map/k,kn->n/dot_general | solution.py:39
  107.3 38.6 %psum.15 = f32[]{:T(128)} all-reduce(f32[]{:T(128)} %get-tuple-element.5), channel_id=1, replica_groups=mesh['rows'=8,'sub'=4] {'rows','sub'}, use_global_device_ids=true, to_apply=%region_6.7 | all-reduce | flops 1 | bytes 8 | tf_op jit(solution)/shard_map/psum | solution.py:40
  146.5 0.7 broadcast_multiply_fusion
  147.2 5.5 %all-to-all-start.1 = ((f32[1,32,512]{2,0,1:T(1,128)}), f32[1,32,512]{2,0,1:T(1,128)S(1)}, u32[]{:S(2)}, u32[]{:S(2)}) async-start(f32[1,32,512]{2,0,1:T(1,128)} %bitcast.15), calls=%async_computation.1 | async-start | bytes 131072 | tf_op jit(solution)/shard_map/all_to_all | solution.py:44
  153.0 6.5 %fusion.17 = f32[40,16384]{1,0:T(8,128)S(1)} fusion(f32[120,40]{0,1:T(8,128)S(1)} %fusion.7, f32[120,16384]{1,0:T(8,128)} %param.5), kind=kOutput, calls=%fused_computation.44 | convolution fusion | flops 943718400 | bytes 10504960 | tf_op jit(solution)/shard_map/kp,kn->pn/dot_general | solution.py:28
  159.5 1.7 copy.31
  161.2 5.8 %all-to-all-start = ((f32[40,32,512]{2,0,1:T(8,128)}), f32[40,32,512]{2,0,1:T(8,128)S(1)}, u32[]{:S(2)}, u32[]{:S(2)}) async-start(f32[40,32,512]{2,0,1:T(8,128)} %bitcast.70), calls=%async_computation | async-start | bytes 5242880 | tf_op jit(solution)/shard_map/all_to_all | solution.py:43
  167.4 67.2 %all_gather.11 = f32[3,120,120]{1,0,2:T(4,128)S(1)} all-gather(f32[3,120,30]{1,0,2:T(4,128)S(1)} %copy.17), channel_id=1, replica_groups=mesh['rows'=8,'sub'=4] {'sub'}, dimensions={2}, use_global_device_ids=true | all-gather | bytes 216000 | tf_op jit(solution)/shard_map/all_gather | solution.py:49
  234.6 0.9 convolution_bitcast_fusion
  235.5 1.0 multiply_reduce_fusion.1
  238.5 0.7 broadcast_select_fusion.1
  239.3 2.2 gather_fusion
  241.5 2.0 copy.21
  243.5 1.7 broadcast_select_fusion
  (31 shorter events, 2.4 us)
Async XLA Ops:
  7.2 145.5 %copy-start = (f32[120,40]{0,1:T(8,128)S(1)}, f32[120,40]{0,1:T(8,128)}, u32[]{:S(2)}) copy-start(f32[120,40]{0,1:T(8,128)} %param.8) | copy-start | bytes 57604
  7.2 10.6 %copy-start.3 = (s32[1,32]{1,0:T(1,128)S(1)}, s32[1,32]{1,0:T(1,128)}, u32[]{:S(2)}) copy-start(s32[1,32]{1,0:T(1,128)} %param.7) | copy-start | bytes 388
  7.2 12.2 %copy-start.1 = (f32[1,16384]{1,0:T(1,128)S(1)}, f32[1,16384]{1,0:T(1,128)}, u32[]{:S(2)}) copy-start(f32[1,16384]{1,0:T(1,128)} %param.6) | copy-start | bytes 196612
  7.2 69.7 %all-gather.3.cloned.1.call-start = ((), (), s32[]{:S(2)}) async-start(), calls=%async_computation.2 | async-start | bytes 2027520 | tf_op jit(solution)/shard_map/all_gather | solution.py:22
  147.2 14.0 %all-to-all-start.1 = ((f32[1,32,512]{2,0,1:T(1,128)}), f32[1,32,512]{2,0,1:T(1,128)S(1)}, u32[]{:S(2)}, u32[]{:S(2)}) async-start(f32[1,32,512]{2,0,1:T(1,128)} %bitcast.15), calls=%async_computation.1 | async-start | bytes 131072 | tf_op jit(solution)/shard_map/all_to_all | solution.py:44
  159.5 7.7 %copy-start.2 = (f32[3,120,30]{1,2,0:T(8,128)S(1)}, f32[3,120,30]{1,2,0:T(8,128)}, u32[]{:S(2)}) copy-start(f32[3,120,30]{1,2,0:T(8,128)} %param.9) | copy-start | bytes 129604
  161.2 78.1 %all-to-all-start = ((f32[40,32,512]{2,0,1:T(8,128)}), f32[40,32,512]{2,0,1:T(8,128)S(1)}, u32[]{:S(2)}, u32[]{:S(2)}) async-start(f32[40,32,512]{2,0,1:T(8,128)} %bitcast.70), calls=%async_computation | async-start | bytes 5242880 | tf_op jit(solution)/shard_map/all_to_all | solution.py:43
Sparse Core Ops, SparseCore 0:
  17.9 58.9 all-gather.2
